TPU v7x, 32 devices: a whole 2x2x4 slice. The times are simulated.
32 devices in a mesh: seq: 8 (over z, y), tp: 4 (over x, core).
Axes of the slice: x: 2, y: 2, z: 4, core: 2. Of those that a mesh axis runs over, the one named last changes fastest.
Arguments:
- tokens: bfloat16 [6144, 4096], P('seq'), may hold values from -6 to 6
- query_weight: bfloat16 [4096, 2048], P('seq', 'tp'), may hold values from -0.09375 to 0.09375
- key_weight: bfloat16 [4096, 2048], P('seq', 'tp'), may hold values from -0.09375 to 0.09375
- value_weight: bfloat16 [4096, 2048], P('seq', 'tp'), may hold values from -0.09375 to 0.09375
- gate_weight: bfloat16 [4096, 16], P('seq', 'tp'), may hold values from -0.09375 to 0.09375
- decay_rate: float32 [16], P('tp'), may hold values from 3.2552085e-05 to 0.04
- norm_gain: float32 [2048], P('tp'), may hold values from 0.5 to 1.5
- out_weight: bfloat16 [2048, 4096], P(None, 'tp'), may hold values from -0.125 to 0.125
Outputs:
- mixed: bfloat16 [6144, 4096], P('seq', 'tp')
All inputs are finite; a program needn't handle non-finite values.
Results may differ from a plain program's by a relative error of at most 0.006.
The roundings to bfloat16 on the way count: a program that leaves them out, or rounds other values in their place, can miss the bound.
Values may be sent and summed in bfloat16 or wider, within the bound.
A program may use at most 128 MiB of HBM per device.

v0:
```python
import jax
import jax.numpy as jnp
from jax import lax
from jax.sharding import PartitionSpec as P


def on_device(
    tokens, query_weight, key_weight, value_weight, gate_weight, decay_rate, norm_gain, out_weight
):
    tok_rows = tokens.shape[0]
    head_count = decay_rate.shape[0]
    proj_width = query_weight.shape[1]
    head_size = proj_width // head_count

    def contract(piece):
        return jnp.dot(tokens, piece, preferred_element_type=jnp.float32)

    query_proj = contract(lax.all_gather(query_weight, "seq", axis=0, tiled=True))
    pieces = (
        lax.all_gather(key_weight, "seq", axis=0, tiled=True),
        lax.all_gather(value_weight, "seq", axis=0, tiled=True),
        lax.all_gather(gate_weight, "seq", axis=0, tiled=True),
    )
    key_proj, value_proj, gate_logit = tuple((contract(one_piece) for one_piece in pieces))
    query_heads = query_proj.astype(jnp.bfloat16).reshape(tok_rows, head_count, head_size)
    key_heads = key_proj.astype(jnp.bfloat16).reshape(tok_rows, head_count, head_size)
    value_per_head = value_proj.astype(jnp.bfloat16).reshape(tok_rows, head_count, head_size)
    log_decay = -decay_rate[None, :] * jax.nn.softplus(gate_logit)
    within = jnp.cumsum(log_decay, axis=0)
    block_total = within[-1]
    key_scaled = (jnp.exp(block_total[None, :] - within)[:, :, None] * key_heads).astype(
        jnp.bfloat16
    )
    shard_local_state = jnp.einsum(
        "gfw,gfz->fwz", key_scaled, value_per_head, preferred_element_type=jnp.float32
    )
    all_totals = lax.all_gather(block_total[None, :], "seq", axis=0, tiled=True)
    running_sum = jnp.cumsum(all_totals, axis=0)
    seq_rank = lax.axis_index("seq")
    before = lax.dynamic_index_in_dim(running_sum, jnp.maximum(seq_rank - 1, 0), 0, keepdims=False)
    piece = lax.all_gather(shard_local_state[None], "seq", axis=0, tiled=True)
    piece_rows = piece.shape[0]
    positions = jnp.arange(piece_rows, dtype=jnp.int32)
    earlier_ok = (positions < seq_rank)[:, None]
    factor = jnp.where(
        earlier_ok, jnp.exp(jnp.where(earlier_ok, before[None, :] - running_sum, 0.0)), 0.0
    )
    prefix_state = jnp.sum(factor[:, :, None, None] * piece, axis=0)
    query_scaled = (jnp.exp(within)[:, :, None] * query_heads).astype(jnp.bfloat16)
    carried_state = jnp.einsum(
        "fys,ysu->fyu",
        query_scaled,
        prefix_state.astype(jnp.bfloat16),
        preferred_element_type=jnp.float32,
    )
    scores = jnp.einsum("thk,shk->hts", query_heads, key_heads, preferred_element_type=jnp.float32)
    row_index = lax.broadcasted_iota(jnp.int32, (tok_rows, tok_rows), 0)
    col_index = lax.broadcasted_iota(jnp.int32, (tok_rows, tok_rows), 1)
    causal = (col_index <= row_index)[None, :, :]
    decay_gap = within.T[:, :, None] - within.T[:, None, :]
    attn = jnp.where(causal, scores * jnp.exp(jnp.where(causal, decay_gap, 0.0)), 0.0).astype(
        jnp.bfloat16
    )
    local_part = jnp.einsum(
        "hts,shv->thv", attn, value_per_head, preferred_element_type=jnp.float32
    )
    head_out = carried_state + local_part
    mean_square = jnp.mean(head_out * head_out, axis=-1, keepdims=True)
    normed = (head_out * lax.rsqrt(mean_square + 1e-05)).reshape(tok_rows, proj_width) * norm_gain[
        None, :
    ]
    normed = normed.astype(jnp.bfloat16)
    mixed = jnp.dot(
        lax.all_gather(normed, "tp", axis=1, tiled=True),
        out_weight,
        preferred_element_type=jnp.float32,
    )
    return mixed.astype(jnp.bfloat16)


def solution(mesh):
    return jax.shard_map(
        on_device,
        mesh=mesh,
        in_specs=(
            P("seq", None),
            P("seq", "tp"),
            P("seq", "tp"),
            P("seq", "tp"),
            P("seq", "tp"),
            P("tp"),
            P("tp"),
            P(None, "tp"),
        ),
        out_specs=P("seq", "tp"),
        check_vma=False,
    )
```

profile of v0, /device:TPU:0, one launch (start us, length us, event | category | flops | bytes accessed | tf_op | source)
XLA Modules:
  0.0 327.7 jit_solution(9326917545958776825)
XLA Ops:
  6.5 0.7 all-gather.8.cloned.1.call-update
  7.3 0.7 all-gather.10.cloned.1.call-update
  8.1 0.7 all-gather.12.cloned.1.call-update
  8.8 0.7 neg.9
  9.4 33.2 %all_gather.21 = bf16[4096,4]{0,1:T(4,128)(2,1)S(1)} all-gather(bf16[512,4]{0,1:T(4,128)(2,1)} %param.12), channel_id=1, replica_groups=mesh['seq'=8,'tp'=4] {'seq'}, dimensions={0}, use_global_device_ids=true | all-gather | bytes 36864 | tf_op jit(solution)/shard_map/all_gather | solution.py:22
  42.7 4.5 %fusion.10 = f32[4,768]{1,0:T(4,128)S(1)} fusion(f32[4]{0:T(128)S(1)} %neg.9, bf16[4096,4]{0,1:T(4,128)(2,1)S(1)} %all_gather.21, bf16[768,4096]{1,0:T(8,128)(2,1)} %param.8), kind=kOutput, calls=%fused_computation.25 | convolution fusion | flops 25187328 | bytes 6336528 | tf_op jit(solution)/shard_map/dot_general | solution.py:16
  47.2 1.1 reduce-window.6
  49.1 36.1 %all-gather.8.cloned.1.call-done = bf16[4096,512]{1,0:T(8,128)(2,1)} async-done(((bf16[512,512]{1,0:T(8,128)(2,1)}), bf16[4096,512]{1,0:T(8,128)(2,1)}) %all-gather.8.cloned.1.call-update) | async-done | bytes 4194320 | tf_op jit(solution)/shard_map/all_gather | solution.py:20
  85.2 7.5 %convolution_convert_fusion.3 = bf16[768,512]{0,1:T(8,128)(2,1)S(1)} fusion(bf16[768,4096]{1,0:T(8,128)(2,1)} %param.8, bf16[4096,512]{1,0:T(8,128)(2,1)} %all-gather.8.cloned.1.call-done), kind=kOutput, calls=%fused_computation.17 | convolution fusion | flops 3221618688 | bytes 11272192 | tf_op jit(solution)/shard_map/dot_general | solution.py:16
  92.7 66.0 %all-gather.10.cloned.1.call-done = bf16[4096,512]{1,0:T(8,128)(2,1)} async-done(((bf16[512,512]{1,0:T(8,128)(2,1)}), bf16[4096,512]{1,0:T(8,128)(2,1)}) %all-gather.10.cloned.1.call-update) | async-done | bytes 4194320 | tf_op jit(solution)/shard_map/all_gather | solution.py:21
  158.7 7.5 %convolution_convert_fusion.2 = bf16[768,512]{0,1:T(8,128)(2,1)S(1)} fusion(bf16[768,4096]{1,0:T(8,128)(2,1)} %param.8, bf16[4096,512]{1,0:T(8,128)(2,1)} %all-gather.10.cloned.1.call-done), kind=kOutput, calls=%fused_computation.16 | convolution fusion | flops 3221618688 | bytes 11272192 | tf_op jit(solution)/shard_map/dot_general | solution.py:16
  166.2 0.9 copy-done.2
  167.0 1.1 fusion.6
  168.2 18.8 %all-gather.1 = f32[8,1,4]{2,1,0:T(1,128)S(1)} all-gather(f32[1,1,4]{2,1,0:T(1,128)S(1)} %bitcast.45), channel_id=1, replica_groups=mesh['seq'=8,'tp'=4] {'seq'}, dimensions={0}, use_global_device_ids=true | all-gather | bytes 144 | tf_op jit(solution)/shard_map/all_gather | solution.py:37
  187.7 1.0 iota_compare_fusion
  188.7 43.6 %all-gather.12.cloned.1.call-done = bf16[4096,512]{1,0:T(8,128)(2,1)} async-done(((bf16[512,512]{1,0:T(8,128)(2,1)}), bf16[4096,512]{1,0:T(8,128)(2,1)}) %all-gather.12.cloned.1.call-update) | async-done | bytes 4194320 | tf_op jit(solution)/shard_map/all_gather | solution.py:18
  232.2 7.5 %convolution_convert_fusion.1 = bf16[768,512]{0,1:T(8,128)(2,1)S(1)} fusion(bf16[768,4096]{1,0:T(8,128)(2,1)} %param.8, bf16[4096,512]{1,0:T(8,128)(2,1)} %all-gather.12.cloned.1.call-done), kind=kOutput, calls=%fused_computation.15 | convolution fusion | flops 3221618688 | bytes 11272192 | tf_op jit(solution)/shard_map/dot_general | solution.py:16
  240.1 5.7 %fusion = f32[4,128,768]{2,1,0:T(8,128)S(1)} fusion(bf16[768,4,128]{0,2,1:T(8,128)(2,1)} %bitcast.49, f32[4,768]{1,0:T(4,128)S(1)} %get-tuple-element.6, pred[768,768]{1,0:T(8,128)(4,1)} %iota_compare_fusion, bf16[768,4,128]{0,2,1:T(8,128)(2,1)S(1)} %bitcast.41, bf16[768,4,128]{0,2,1:T(8,128)(2,1)} %bitcast.47), kind=kOutput, calls=%fused_computation.1 | convolution fusion | flops 1219756032 | bytes 4534272 | tf_op jit(solution)/shard_map/hts,shv->thv/dot_general | solution.py:64
  245.8 36.0 %all-gather.16.cloned.1.call-done = f32[32,128,128]{2,1,0:T(8,128)} async-done(((f32[4,128,128]{2,1,0:T(8,128)}), f32[32,128,128]{2,1,0:T(8,128)}) %all-gather.16.cloned.1.call-update) | async-done | bytes 2097168 | tf_op jit(solution)/shard_map/all_gather | solution.py:41
  281.9 1.8 multiply_reduce_fusion
  283.7 1.3 fusion.5
  285.2 1.0 fusion.4
  286.2 27.2 %all-gather.14.cloned.1.call-done = bf16[768,2048]{0,1:T(8,128)(2,1)} async-done(((bf16[768,512]{0,1:T(8,128)(2,1)}), bf16[768,2048]{0,1:T(8,128)(2,1)}) %all-gather.14.cloned.1.call-update) | async-done | bytes 3145744 | tf_op jit(solution)/shard_map/all_gather | solution.py:74
  313.4 7.8 %convolution_convert_fusion = bf16[768,1024]{1,0:T(8,128)(2,1)} fusion(bf16[768,2048]{0,1:T(8,128)(2,1)} %all-gather.14.cloned.1.call-done, bf16[2048,1024]{1,0:T(8,128)(2,1)} %param.15), kind=kOutput, calls=%fused_computation.6 | convolution fusion | flops 3222011904 | bytes 8912896 | tf_op jit(solution)/shard_map/dot_general | solution.py:73
  (28 shorter events, 2.0 us)
Async XLA Ops:
  6.5 78.7 %all-gather.8.cloned.1.call-start = ((), (), s32[]{:S(2)}) async-start(), calls=%async_computation | async-start | bytes 4718592 | tf_op jit(solution)/shard_map/all_gather | solution.py:20
  7.3 151.4 %all-gather.10.cloned.1.call-start = ((), (), s32[]{:S(2)}) async-start(), calls=%async_computation.1 | async-start | bytes 4718592 | tf_op jit(solution)/shard_map/all_gather | solution.py:21
  8.0 224.2 %all-gather.12.cloned.1.call-start = ((), (), s32[]{:S(2)}) async-start(), calls=%async_computation.2 | async-start | bytes 4718592 | tf_op jit(solution)/shard_map/all_gather | solution.py:18
  8.7 273.1 %all-gather.16.cloned.1.call-start = ((), (), s32[]{:S(2)}) async-start(), calls=%async_computation.4 | async-start | bytes 2359296 | tf_op jit(solution)/shard_map/all_gather | solution.py:41
  92.7 73.5 %copy-start.1 = (bf16[768,512]{0,1:T(8,128)(2,1)}, bf16[768,512]{0,1:T(8,128)(2,1)S(1)}, u32[]{:S(2)}) copy-start(bf16[768,512]{0,1:T(8,128)(2,1)S(1)} %convolution_convert_fusion.3) | copy-start | bytes 2359300
  166.2 0.9 copy-start.2
  168.2 145.2 %all-gather.14.cloned.1.call-start = ((), (), s32[]{:S(2)}) async-start(), calls=%async_computation.3 | async-start | bytes 3932160 | tf_op jit(solution)/shard_map/all_gather | solution.py:74
  283.7 1.5 copy-start
Sparse Core Ops, SparseCore 0:
  9.5 75.6 all-gather.7
  87.3 71.3 all-gather.9
  160.8 71.3 all-gather.11
  234.2 47.5 all-gather.15
  286.3 27.0 all-gather.13
where the time goes:
time: 328 us
  waiting for transfers between devices  211 us (64%)
  blocking collectives  52.1 us (16%)
  matrix products  42.8 us (13%)
  between operations  13.3 us (4%)
  other arithmetic  6.38 us (2%)
    all_gather x1, waiting for transfers between devices, on_device(): lax.all_gather(value_weight, 'seq', axis=0, tiled=True)  66 us
    all_gather x1, waiting for transfers between devices, on_device(): lax.all_gather(query_weight, 'seq', axis=0, tiled=True)  43.6 us
    all_gather x1, waiting for transfers between devices, on_device(): lax.all_gather(key_weight, 'seq', axis=0, tiled=True)  36.1 us
    all_gather x1, waiting for transfers between devices, on_device(): piece = lax.all_gather(shard_local_state[None], 'seq', axis=0, tiled=True)  36 us
    all_gather x1, blocking collectives, on_device(): lax.all_gather(gate_weight, 'seq', axis=0, tiled=True)  33.2 us
    all_gather x1, waiting for transfers between devices, on_device(): lax.all_gather(normed, 'tp', axis=1, tiled=True)  27.2 us
    dot_general x4, matrix products, contract(): return jnp.dot(tokens, piece, preferred_element_type=jnp.float32)  26.9 us
    all_gather x1, blocking collectives, on_device(): all_totals = lax.all_gather(block_total[None, :], 'seq', axis=0, tiled=True)  18.8 us
  transfers between devices with their start and end apart: 5, of which 5 were waited for; matrix products, arithmetic and copies ran while one was open for 12% of the time, Pallas kernels for 0%

commit v1 on v0

--- a/solution.py
+++ b/solution.py
@@ -1,30 +1,285 @@
+import functools
+
 import jax
 import jax.numpy as jnp
 from jax import lax
+from jax.experimental import pallas as pl
+from jax.experimental.pallas import tpu as pltpu
 from jax.sharding import PartitionSpec as P
 
+HALVES = 2
+MESH = pl.DeviceIdType.MESH
+
+
+def project_kernel(seq, wide, *refs):
+    tok_ref, gate_in, key_in, value_in, query_in = refs[:5]
+    gate_out, key_out, value_out, query_out = refs[5:9]
+    gate_buf, kvq_buf, gate_acc, acc, own_sem, send_own, send_line, send_peer, recv_sem = refs[9:]
+    rows = key_in.shape[0]
+    half = key_in.shape[1] // HALVES
+    cross = 2
+    line = seq // cross
+    me = lax.axis_index("seq")
+    a, b = me // cross, me % cross
+    peer = a * cross + (1 - b)
+
+    def buffer(piece, source):
+        if piece == 0:
+            return gate_buf.at[source]
+        return kvq_buf.at[piece - 1, source]
+
+    def tok(source):
+        if wide:
+            return tok_ref[:, pl.ds(pl.multiple_of(source * rows, rows), rows)]
+        return tok_ref[source]
+
+    def copy(piece, source, sem, target):
+        return pltpu.make_async_remote_copy(
+            src_ref=buffer(piece, source),
+            dst_ref=buffer(piece, source),
+            send_sem=sem,
+            recv_sem=recv_sem.at[piece, source],
+            device_id={"seq": target},
+            device_id_type=MESH,
+        )
+
+    def arrive(piece, source):
+        copy(piece, source, send_own.at[piece, 0], peer).wait_recv()
+
+    phases = [[1, 0, 2, 3], [4, 5, 6]]
+    peer_first = (1,)
+
+    loads = [pltpu.make_async_copy(gate_in, gate_buf.at[me], own_sem.at[0])]
+    for index in range(3 * HALVES):
+        source_ref = (key_in, value_in, query_in)[index % 3]
+        at = (index // 3) * half
+        loads.append(
+            pltpu.make_async_copy(
+                source_ref.at[:, pl.ds(at, half)], kvq_buf.at[index, me], own_sem.at[index + 1]
+            )
+        )
+    for load in loads:
+        load.start()
+
+    barrier = pltpu.get_barrier_semaphore()
+    has_up, has_down = a < line - 1, a > 0
+    pl.semaphore_signal(barrier, inc=1, device_id={"seq": peer}, device_id_type=MESH)
+
+    @pl.when(has_up)
+    def _():
+        pl.semaphore_signal(barrier, inc=1, device_id={"seq": me + cross}, device_id_type=MESH)
+
+    @pl.when(has_down)
+    def _():
+        pl.semaphore_signal(barrier, inc=1, device_id={"seq": me - cross}, device_id_type=MESH)
+
+    pl.semaphore_wait(barrier, 1 + has_up.astype(jnp.int32) + has_down.astype(jnp.int32))
+
+    def send_mine(pieces):
+        for piece in pieces:
+            loads[piece].wait()
+            copy(piece, me, send_own.at[piece, 0], peer).start()
+
+            @pl.when(has_up)
+            def _():
+                copy(piece, me, send_own.at[piece, 1], me + cross).start()
+
+            @pl.when(has_down)
+            def _():
+                copy(piece, me, send_own.at[piece, 2], me - cross).start()
+
+    def multiply(piece, source):
+        x = tok(source)
+        if piece == 0:
+            gate_acc[...] += lax.dot_general(
+                x, gate_buf[source], (((1,), (1,)), ((), ())), preferred_element_type=jnp.float32
+            )
+        else:
+            acc[piece - 1] += jnp.dot(
+                x, kvq_buf[piece - 1, source], preferred_element_type=jnp.float32
+            )
+
+    def step_of(t):
+        d = 1 + t // 2
+        sign = 1 - 2 * (t % 2)
+        origin = a - sign * d
+        ahead = a + sign
+        valid = (origin >= 0) & (origin < line)
+        onward = valid & (ahead >= 0) & (ahead < line)
+        return origin, valid, onward, me + sign * cross
+
+    def from_peer(pieces, t):
+        origin, valid, _, _ = step_of(t)
+
+        @pl.when(valid)
+        def _():
+            source = origin * cross + (1 - b)
+            for piece in pieces:
+                if piece not in peer_first:
+                    arrive(piece, source)
+                multiply(piece, source)
+
+    gate_acc[...] = jnp.zeros_like(gate_acc)
+    acc[...] = jnp.zeros_like(acc)
+    steps = 2 * (line - 1)
+    for number, pieces in enumerate(phases):
+        if number == 0:
+            send_mine(pieces)
+        for piece in pieces:
+            if piece in peer_first:
+                arrive(piece, peer)
+
+                @pl.when(has_up)
+                def _():
+                    copy(piece, peer, send_line.at[piece, peer], me + cross).start()
+
+                @pl.when(has_down)
+                def _():
+                    copy(piece, peer, send_peer.at[piece, peer], me - cross).start()
+
+        for piece in pieces:
+            multiply(piece, me)
+
+        @pl.loop(0, steps)
+        def _(t):
+            origin, valid, onward, target = step_of(t)
+            source = origin * cross + b
+            other = origin * cross + (1 - b)
+
+            @pl.when(valid)
+            def _():
+                for piece in pieces:
+                    arrive(piece, source)
+
+                    @pl.when(onward)
+                    def _():
+                        copy(piece, source, send_line.at[piece, source], target).start()
+
+                    if piece in peer_first:
+                        arrive(piece, other)
+
+                        @pl.when(onward)
+                        def _():
+                            copy(piece, other, send_line.at[piece, other], target).start()
+                    else:
+                        copy(piece, source, send_peer.at[piece, source], peer).start()
+                for piece in pieces:
+                    multiply(piece, source)
+
+            @pl.when(t == 1)
+            def _():
+                for piece in pieces:
+                    if piece not in peer_first:
+                        arrive(piece, peer)
+                    multiply(piece, peer)
+
+            @pl.when(t >= 2)
+            def _():
+                from_peer(pieces, t - 2)
+
+        if number + 1 < len(phases):
+            send_mine(phases[number + 1])
+
+        @pl.loop(steps - 2, steps)
+        def _(t):
+            from_peer(pieces, t)
+
+    gate_out[...] = gate_acc[...]
+    for index in range(3 * HALVES):
+        out = (key_out, value_out, query_out)[index % 3]
+        at = (index // 3) * half
+        out[:, pl.ds(at, half)] = acc[index].astype(jnp.bfloat16)
+
+    for pieces in phases:
+        for piece in pieces:
+            copy(piece, me, send_own.at[piece, 0], peer).wait_send()
+
+            @pl.when(has_up)
+            def _():
+                copy(piece, me, send_own.at[piece, 1], peer).wait_send()
+
+            @pl.when(has_down)
+            def _():
+                copy(piece, me, send_own.at[piece, 2], peer).wait_send()
+
+            if piece in peer_first:
+
+                @pl.when(has_up)
+                def _():
+                    copy(piece, peer, send_line.at[piece, peer], peer).wait_send()
+
+                @pl.when(has_down)
+                def _():
+                    copy(piece, peer, send_peer.at[piece, peer], peer).wait_send()
+
+        @pl.loop(0, steps)
+        def _(t):
+            origin, valid, onward, target = step_of(t)
+            source = origin * cross + b
+            other = origin * cross + (1 - b)
+            for piece in pieces:
+
+                @pl.when(onward)
+                def _():
+                    copy(piece, source, send_line.at[piece, source], peer).wait_send()
+                    if piece in peer_first:
+                        copy(piece, other, send_line.at[piece, other], peer).wait_send()
+
+                if piece not in peer_first:
+
+                    @pl.when(valid)
+                    def _():
+                        copy(piece, source, send_peer.at[piece, source], peer).wait_send()
+
+
+def project(seq, tokens, query_weight, key_weight, value_weight, gate_weight):
+    count = tokens.shape[0]
+    rows, width = query_weight.shape
+    heads = gate_weight.shape[1]
+    wide = rows % 128 == 0
+    tok = tokens if wide else tokens.reshape(count, seq, rows).transpose(1, 0, 2)
+    gate_t = jnp.pad(gate_weight.T, ((0, 16 - heads), (0, 0)))
+    vmem = pl.BlockSpec(memory_space=pltpu.VMEM)
+    hbm = pl.BlockSpec(memory_space=pl.ANY)
+    pieces = 3 * HALVES + 1
+    wide_out = jax.ShapeDtypeStruct((count, width), jnp.bfloat16)
+    dma = pltpu.SemaphoreType.DMA
+    return pl.pallas_call(
+        functools.partial(project_kernel, seq, wide),
+        out_shape=(jax.ShapeDtypeStruct((count, 16), jnp.float32), wide_out, wide_out, wide_out),
+        in_specs=[vmem, hbm, hbm, hbm, hbm],
+        out_specs=(vmem, vmem, vmem, vmem),
+        scratch_shapes=[
+            pltpu.VMEM((seq, 16, rows), jnp.bfloat16),
+            pltpu.VMEM((3 * HALVES, seq, rows, width // HALVES), jnp.bfloat16),
+            pltpu.VMEM((count, 16), jnp.float32),
+            pltpu.VMEM((3 * HALVES, count, width // HALVES), jnp.float32),
+            dma((pieces,)),
+            dma((pieces, 3)),
+            dma((pieces, seq)),
+            dma((pieces, seq)),
+            dma((pieces, seq)),
+        ],
+        compiler_params=pltpu.CompilerParams(
+            collective_id=0, has_side_effects=True, vmem_limit_bytes=60 * 1024 * 1024
+        ),
+    )(tok, gate_t, key_weight, value_weight, query_weight)
+
 
 def on_device(
-    tokens, query_weight, key_weight, value_weight, gate_weight, decay_rate, norm_gain, out_weight
+    seq, tokens, query_weight, key_weight, value_weight, gate_weight, decay_rate, norm_gain, out_weight
 ):
     tok_rows = tokens.shape[0]
     head_count = decay_rate.shape[0]
     proj_width = query_weight.shape[1]
     head_size = proj_width // head_count
-
-    def contract(piece):
-        return jnp.dot(tokens, piece, preferred_element_type=jnp.float32)
-
-    query_proj = contract(lax.all_gather(query_weight, "seq", axis=0, tiled=True))
-    pieces = (
-        lax.all_gather(key_weight, "seq", axis=0, tiled=True),
-        lax.all_gather(value_weight, "seq", axis=0, tiled=True),
-        lax.all_gather(gate_weight, "seq", axis=0, tiled=True),
-    )
-    key_proj, value_proj, gate_logit = tuple((contract(one_piece) for one_piece in pieces))
-    query_heads = query_proj.astype(jnp.bfloat16).reshape(tok_rows, head_count, head_size)
-    key_heads = key_proj.astype(jnp.bfloat16).reshape(tok_rows, head_count, head_size)
-    value_per_head = value_proj.astype(jnp.bfloat16).reshape(tok_rows, head_count, head_size)
+    gate_wide, key_proj, value_proj, query_proj = project(
+        seq, tokens, query_weight, key_weight, value_weight, gate_weight
+    )
+    gate_logit = gate_wide[:, :head_count]
+    query_heads = query_proj.reshape(tok_rows, head_count, head_size)
+    key_heads = key_proj.reshape(tok_rows, head_count, head_size)
+    value_per_head = value_proj.reshape(tok_rows, head_count, head_size)
     log_decay = -decay_rate[None, :] * jax.nn.softplus(gate_logit)
     within = jnp.cumsum(log_decay, axis=0)
     block_total = within[-1]
@@ -80,7 +335,7 @@
 
 def solution(mesh):
     return jax.shard_map(
-        on_device,
+        functools.partial(on_device, mesh.shape["seq"]),
         mesh=mesh,
         in_specs=(
             P("seq", None),

time: 328 us -> 265 us (0.81)
  waiting for transfers between devices: 211 us -> 50 us
  Pallas kernels: 0 us -> 157 us
  blocking collectives: 52.1 us -> 17 us
  matrix products: 42.8 us -> 15.2 us
    pallas_call x0 -> x1, Pallas kernels: none -> 157 us  [project(): pl.pallas_call(functools.partial(project_kernel, seq, wide), out_shape=(j...]
    all_gather x3 -> x0, waiting for transfers between devices: 146 us -> none  [the longest x1 66 us: on_device(): lax.all_gather(value_weight, 'seq', axis=0, tiled=True)]
    all_gather x1 -> x0, blocking collectives: 33.2 us -> none  [on_device(): lax.all_gather(gate_weight, 'seq', axis=0, tiled=True)]
    dot_general x4 -> x0, matrix products: 26.9 us -> none  [contract(): return jnp.dot(tokens, piece, preferred_element_type=jnp.float32)]
    all_gather x1, waiting for transfers between devices: 36 us -> 22.8 us  [on_device(): piece = lax.all_gather(shard_local_state[None], 'seq', axis=0, tiled=True)]
  transfers between devices with their start and end apart: 5 -> 2, of which waited for: 5 -> 2; matrix products, arithmetic and copies ran while one was open for 12% -> 3% of each run, Pallas kernels for 0% -> 0%
where the time goes in v1:
time: 265 us
  Pallas kernels  157 us (59%)
  waiting for transfers between devices  50 us (19%)
  blocking collectives  17 us (6%)
  matrix products  15.2 us (6%)
  between operations  13.5 us (5%)
  other arithmetic  6.93 us (3%)
  local copies, waits for them, and re-layouts  4.5 us (2%)
    pallas_call x1, Pallas kernels, project(): pl.pallas_call(functools.partial(project_kernel, seq, wide), out_shape=(j...  157 us
    all_gather x1, waiting for transfers between devices, on_device(): lax.all_gather(normed, 'tp', axis=1, tiled=True)  27.2 us
    all_gather x1, waiting for transfers between devices, on_device(): piece = lax.all_gather(shard_local_state[None], 'seq', axis=0, tiled=True)  22.8 us
    all_gather x1, blocking collectives, on_device(): all_totals = lax.all_gather(block_total[None, :], 'seq', axis=0, tiled=True)  17 us
    dot_general x1, matrix products, on_device(): jnp.dot(lax.all_gather(normed, 'tp', axis=1, tiled=True), out_weight, pre...  7.75 us
  transfers between devices with their start and end apart: 2, of which 2 were waited for; matrix products, arithmetic and copies ran while one was open for 3% of the time, Pallas kernels for 0%

profile of v1, /device:TPU:0, one launch (start us, length us, event | category | flops | bytes accessed | tf_op | source)
XLA Modules:
  0.0 264.6 jit_solution(14368854254233806933)
XLA Ops:
  6.5 1.3 pad.4.refs_1_
  7.8 157.4 %shard_map.82 = (f32[768,16]{1,0:T(8,128)}, bf16[768,512]{1,0:T(8,128)(2,1)}, bf16[768,512]{1,0:T(8,128)(2,1)}, bf16[768,512]{1,0:T(8,128)(2,1)}) custom-call(bf16[768,4096]{1,0:T(8,128)(2,1)} %refs_0_.1, bf16[16,512]{1,0:T(8,128)(2,1)} %pad.4.refs_1_, bf16[512,512]{1,0:T(8,128)(2,1)} %refs_2_.1, bf16[512,512]{1,0:T(8,128)(2,1)} %refs_3_.1, ...), custom_call_target="tpu_custom_call" | custom-call | tf_op jit(solution)/shard_map/pallas_call | solution.py:247
  165.2 1.5 copy.47
  166.7 1.2 fusion.15
  168.0 0.2 copy.35
  168.2 1.1 reduce-window.6
  169.3 0.2 slice_reduce_fusion
  169.5 0.2 reduce-window.9
  169.7 0.3 copy.46
  170.0 0.2 slice_reduce_fusion.1
  170.3 1.1 fusion.6
  171.5 17.0 %all-gather.1 = f32[8,1,4]{2,1,0:T(1,128)S(1)} all-gather(f32[1,1,4]{2,1,0:T(1,128)S(1)} %bitcast.60), channel_id=1, replica_groups=mesh['seq'=8,'tp'=4] {'seq'}, dimensions={0}, use_global_device_ids=true | all-gather | bytes 144 | tf_op jit(solution)/shard_map/all_gather | solution.py:292
  188.6 0.2 reduce_window_sum.36
  188.7 0.2 dynamic-slice_reduce_fusion
  189.1 1.0 iota_compare_fusion
  190.1 5.1 %fusion = f32[4,128,768]{2,1,0:T(8,128)S(1)} fusion(bf16[768,4,128]{0,2,1:T(8,128)(2,1)S(1)} %bitcast.54, f32[4,768]{1,0:T(4,128)S(1)} %get-tuple-element.14, pred[768,768]{1,0:T(8,128)(4,1)} %iota_compare_fusion, bf16[768,4,128]{0,2,1:T(8,128)(2,1)S(1)} %bitcast.56, bf16[768,512]{1,0:T(8,128)(2,1)} %get-tuple-element.12), kind=kOutput, calls=%fused_computation.1 | convolution fusion | flops 1219756032 | bytes 4534272 | tf_op jit(solution)/shard_map/hts,shv->thv/dot_general | solution.py:319
  195.2 22.8 %all-gather.7.cloned.1.call-done = f32[32,128,128]{2,1,0:T(8,128)} async-done(((f32[4,128,128]{2,1,0:T(8,128)}), f32[32,128,128]{2,1,0:T(8,128)}) %all-gather.7.cloned.1.call-update) | async-done | bytes 2097168 | tf_op jit(solution)/shard_map/all_gather | solution.py:296
  218.0 1.8 multiply_reduce_fusion
  219.8 1.3 fusion.5
  221.1 0.1 bitcast_multiply_fusion.1
  221.3 0.5 copy-done.2
  221.8 1.0 fusion.4
  222.8 27.2 %all-gather.5.cloned.1.call-done = bf16[768,2048]{0,1:T(8,128)(2,1)} async-done(((bf16[768,512]{0,1:T(8,128)(2,1)}), bf16[768,2048]{0,1:T(8,128)(2,1)}) %all-gather.5.cloned.1.call-update) | async-done | bytes 3145744 | tf_op jit(solution)/shard_map/all_gather | solution.py:329
  250.0 7.8 %convolution_convert_fusion = bf16[768,1024]{1,0:T(8,128)(2,1)} fusion(bf16[768,2048]{0,1:T(8,128)(2,1)} %all-gather.5.cloned.1.call-done, bf16[2048,1024]{1,0:T(8,128)(2,1)} %param.15), kind=kOutput, calls=%fused_computation.6 | convolution fusion | flops 3222011904 | bytes 8912896 | tf_op jit(solution)/shard_map/dot_general | solution.py:328
  (20 shorter events, 0.5 us)
Async XLA Ops:
  6.5 211.4 %all-gather.7.cloned.1.call-start = ((), (), s32[]{:S(2)}) async-start(), calls=%async_computation.1 | async-start | bytes 2359296 | tf_op jit(solution)/shard_map/all_gather | solution.py:296
  7.8 158.9 %copy-start.3 = (f32[4]{0:T(128)S(1)}, f32[4]{0:T(128)}, u32[]{:S(2)}) copy-start(f32[4]{0:T(128)} %param.13) | copy-start | bytes 52
  165.2 4.5 %copy-start = (bf16[768,512]{1,0:T(8,128)(2,1)S(1)}, bf16[768,512]{1,0:T(8,128)(2,1)}, u32[]{:S(2)}) copy-start(bf16[768,512]{1,0:T(8,128)(2,1)} %get-tuple-element.10) | copy-start | bytes 2359300
  171.4 78.6 %all-gather.5.cloned.1.call-start = ((), (), s32[]{:S(2)}) async-start(), calls=%async_computation | async-start | bytes 3932160 | tf_op jit(solution)/shard_map/all_gather | solution.py:329
  195.2 24.6 %copy-start.1 = (bf16[768,512]{1,0:T(8,128)(2,1)S(1)}, bf16[768,512]{1,0:T(8,128)(2,1)}, u32[]{:S(2)}) copy-start(bf16[768,512]{1,0:T(8,128)(2,1)} %get-tuple-element.12) | copy-start | bytes 2359300
  221.1 0.7 copy-start.2
Sparse Core Ops, SparseCore 0:
  171.5 46.3 all-gather.6
  223.0 27.0 all-gather.4

commit v2 on v1

--- a/solution.py
+++ b/solution.py
@@ -11,10 +11,13 @@
 MESH = pl.DeviceIdType.MESH
 
 
-def project_kernel(seq, wide, *refs):
-    tok_ref, gate_in, key_in, value_in, query_in = refs[:5]
-    gate_out, key_out, value_out, query_out = refs[5:9]
-    gate_buf, kvq_buf, gate_acc, acc, own_sem, send_own, send_line, send_peer, recv_sem = refs[9:]
+def layer_kernel(seq, tp, heads, wide, *refs):
+    tok_ref, rate_ref, gain_ref, gate_in, key_in, value_in, query_in, out_in = refs[:8]
+    mixed_ref = refs[8]
+    gate_buf, kvq_buf, gate_acc, acc, out_buf, out_acc, wcol, wrow = refs[9:17]
+    state_mine, state_peer, state_in, state_next, normed_buf = refs[17:22]
+    own_sem, send_own, send_line, send_peer, recv_sem = refs[22:27]
+    state_send, state_recv, normed_send, normed_recv = refs[27:31]
     rows = key_in.shape[0]
     half = key_in.shape[1] // HALVES
     cross = 2
@@ -22,6 +25,14 @@
     me = lax.axis_index("seq")
     a, b = me // cross, me % cross
     peer = a * cross + (1 - b)
+    count = acc.shape[1]
+    head_size = 2 * half // heads
+    per_half = heads // HALVES
+    block = 256 if count % 256 == 0 else count
+    blocks = count // block
+    col = lax.axis_index("tp")
+    pair_col = col + 1 - 2 * (col % 2)
+    groups = tp // 2
 
     def buffer(piece, source):
         if piece == 0:
@@ -46,7 +57,7 @@
     def arrive(piece, source):
         copy(piece, source, send_own.at[piece, 0], peer).wait_recv()
 
-    phases = [[1, 0, 2, 3], [4, 5, 6]]
+    phases = [[1, 0, 2, 3], [4, 5], [6]]
     peer_first = (1,)
 
     loads = [pltpu.make_async_copy(gate_in, gate_buf.at[me], own_sem.at[0])]
@@ -60,6 +71,8 @@
         )
     for load in loads:
         load.start()
+    out_load = pltpu.make_async_copy(out_in, out_buf, own_sem.at[3 * HALVES + 1])
+    out_load.start()
 
     barrier = pltpu.get_barrier_semaphore()
     has_up, has_down = a < line - 1, a > 0
@@ -73,7 +86,12 @@
     def _():
         pl.semaphore_signal(barrier, inc=1, device_id={"seq": me - cross}, device_id_type=MESH)
 
-    pl.semaphore_wait(barrier, 1 + has_up.astype(jnp.int32) + has_down.astype(jnp.int32))
+    pl.semaphore_signal(barrier, inc=1, device_id={"tp": pair_col}, device_id_type=MESH)
+    for g in range(1, groups):
+        pl.semaphore_signal(
+            barrier, inc=1, device_id={"tp": lax.rem(col + 2 * g, tp)}, device_id_type=MESH
+        )
+    pl.semaphore_wait(barrier, 1 + groups + has_up.astype(jnp.int32) + has_down.astype(jnp.int32))
 
     def send_mine(pieces):
         for piece in pieces:
@@ -119,6 +137,171 @@
                     arrive(piece, source)
                 multiply(piece, source)
 
+    lo_state = per_half * head_size
+
+    def decays():
+        logits = jnp.concatenate(
+            [gate_acc[...], jnp.zeros((count, 128 - gate_acc.shape[1]), jnp.float32)], axis=1
+        ).T[:8]
+        soft = jnp.maximum(logits, 0.0) + jnp.log1p(jnp.exp(-jnp.abs(logits)))
+        total = -rate_ref[...] * soft
+        lane = lax.broadcasted_iota(jnp.int32, total.shape, 1)
+        reach = 1
+        while reach < count:
+            total = total + jnp.where(lane >= reach, pltpu.roll(total, reach, 1), 0.0)
+            reach *= 2
+        wrow[...] = total
+        wcol[...] = jnp.concatenate(
+            [total, jnp.zeros((120, count), jnp.float32)], axis=0
+        ).T
+
+    def state_copy(ref_from, ref_to, h, send, recv, target):
+        return pltpu.make_async_remote_copy(
+            src_ref=ref_from.at[h],
+            dst_ref=ref_to.at[h],
+            send_sem=state_send.at[send, h],
+            recv_sem=state_recv.at[recv, h],
+            device_id={"seq": target},
+            device_id_type=MESH,
+        )
+
+    def pair_state(h):
+        return state_copy(state_mine, state_peer, h, 0, 0, peer)
+
+    def line_state(h):
+        return state_copy(state_next, state_in, h, 1, 1, me + cross)
+
+    def back_state(h):
+        return state_copy(state_in, state_in, h, 2, 1, peer)
+
+    def local_state(h):
+        for j in range(per_half):
+            head = h * per_half + j
+            cols = slice(j * head_size, (j + 1) * head_size)
+            within = wcol[:, head : head + 1]
+            last = wcol[count - 1 : count, head : head + 1]
+            key = acc[3 * h, :, cols].astype(jnp.bfloat16).astype(jnp.float32)
+            scaled = (jnp.exp(last - within) * key).astype(jnp.bfloat16)
+            value = acc[3 * h + 1, :, cols].astype(jnp.bfloat16)
+            state_mine[h, j * head_size : (j + 1) * head_size] = lax.dot_general(
+                scaled, value, (((0,), (0,)), ((), ())), preferred_element_type=jnp.float32
+            )
+            state_mine[h, lo_state + j : lo_state + j + 1] = jnp.broadcast_to(last, (1, head_size))
+
+        @pl.when(b == 0)
+        def _():
+            pair_state(h).start()
+
+        @pl.when(a == 0)
+        def _():
+            state_in[h] = jnp.zeros(state_in.shape[1:], jnp.float32)
+
+    def chain(h):
+        @pl.when(b == 1)
+        def _():
+            pair_state(h).wait_recv()
+
+            @pl.when(has_down)
+            def _():
+                line_state(h).wait_recv()
+                back_state(h).start()
+
+            for j in range(per_half):
+                at = slice(j * head_size, (j + 1) * head_size)
+                tot = slice(lo_state + j, lo_state + j + 1)
+                before = jnp.exp(state_peer[h, tot]) * state_in[h, at] + state_peer[h, at]
+                state_peer[h, at] = before
+                state_next[h, at] = jnp.exp(state_mine[h, tot]) * before + state_mine[h, at]
+
+            @pl.when(has_up)
+            def _():
+                line_state(h).start()
+
+    def chain_end(h):
+        @pl.when(b == 0)
+        def _():
+            @pl.when(has_down)
+            def _():
+                back_state(h).wait_recv()
+
+            state_peer[h, :lo_state] = state_in[h]
+
+    def normed_copy(h, i, source, send, target):
+        at = pl.ds(i * block, block)
+        return pltpu.make_async_remote_copy(
+            src_ref=normed_buf.at[h, source, at],
+            dst_ref=normed_buf.at[h, source, at],
+            send_sem=normed_send.at[h, i, send],
+            recv_sem=normed_recv.at[h, i, source],
+            device_id={"tp": target},
+            device_id_type=MESH,
+        )
+
+    def far(g):
+        return lax.rem(col + 2 * g, tp)
+
+    def far_pair(g):
+        return lax.rem(pair_col + 2 * g, tp)
+
+    def attention(h):
+        for i in range(blocks):
+            t_at = slice(i * block, (i + 1) * block)
+            upto = (i + 1) * block
+            row = i * block + lax.broadcasted_iota(jnp.int32, (block, upto), 0)
+            causal = lax.broadcasted_iota(jnp.int32, (block, upto), 1) <= row
+            for j in range(per_half):
+                head = h * per_half + j
+                cols = slice(j * head_size, (j + 1) * head_size)
+                query = acc[3 * h + 2, t_at, cols].astype(jnp.bfloat16)
+                key = acc[3 * h, :upto, cols].astype(jnp.bfloat16)
+                value = acc[3 * h + 1, :upto, cols].astype(jnp.bfloat16)
+                within = wcol[t_at, head : head + 1]
+                scores = lax.dot_general(
+                    query, key, (((1,), (1,)), ((), ())), preferred_element_type=jnp.float32
+                )
+                gap = within - wrow[head : head + 1, :upto]
+                attn = jnp.where(causal, scores * jnp.exp(jnp.where(causal, gap, 0.0)), 0.0)
+                local = jnp.dot(
+                    attn.astype(jnp.bfloat16), value, preferred_element_type=jnp.float32
+                )
+                scaled = (jnp.exp(within) * query.astype(jnp.float32)).astype(jnp.bfloat16)
+                state = state_peer[h, j * head_size : (j + 1) * head_size].astype(jnp.bfloat16)
+                head_out = local + jnp.dot(scaled, state, preferred_element_type=jnp.float32)
+                square = jnp.mean(head_out * head_out, axis=-1, keepdims=True)
+                gain = gain_ref[:, head * head_size : (head + 1) * head_size]
+                normed_buf[h, col, t_at, cols] = (
+                    head_out * lax.rsqrt(square + 1e-05) * gain
+                ).astype(jnp.bfloat16)
+            for g in range(1, groups):
+                normed_copy(h, i, col, g, far(g)).start()
+            normed_copy(h, i, col, 0, pair_col).start()
+
+    def relay(h, i):
+        for g in range(1, groups):
+            normed_copy(h, i, far(g), 0, pair_col).wait_recv()
+            normed_copy(h, i, far(g), groups - 1 + g, pair_col).start()
+
+    def mix(h, i, source):
+        at = pl.ds(i * block, block)
+        depth = pl.ds(pl.multiple_of((source * HALVES + h) * half, half), half)
+        return jnp.dot(
+            normed_buf[h, source, at], out_buf[depth, :], preferred_element_type=jnp.float32
+        )
+
+    def settle(h, i):
+        at = pl.ds(i * block, block)
+        total = mix(h, i, col)
+        normed_copy(h, i, pair_col, 0, pair_col).wait_recv()
+        total = total + mix(h, i, pair_col)
+        for g in range(1, groups):
+            total = total + mix(h, i, far(g))
+            normed_copy(h, i, far_pair(g), 0, pair_col).wait_recv()
+            total = total + mix(h, i, far_pair(g))
+        if h == 0:
+            out_acc[at, :] = total
+        else:
+            mixed_ref[at, :] = (out_acc[at, :] + total).astype(jnp.bfloat16)
+
     gate_acc[...] = jnp.zeros_like(gate_acc)
     acc[...] = jnp.zeros_like(acc)
     steps = 2 * (line - 1)
@@ -166,6 +349,12 @@
                 for piece in pieces:
                     multiply(piece, source)
 
+            if number >= 1:
+
+                @pl.when(t == 2 * (jnp.maximum(a, 1) - 1))
+                def _():
+                    chain(number - 1)
+
             @pl.when(t == 1)
             def _():
                 for piece in pieces:
@@ -184,11 +373,43 @@
         def _(t):
             from_peer(pieces, t)
 
-    gate_out[...] = gate_acc[...]
-    for index in range(3 * HALVES):
-        out = (key_out, value_out, query_out)[index % 3]
-        at = (index // 3) * half
-        out[:, pl.ds(at, half)] = acc[index].astype(jnp.bfloat16)
+        if number == 0:
+            decays()
+            local_state(0)
+        elif number == 1:
+            local_state(1)
+            chain_end(0)
+            attention(0)
+
+    for i in range(blocks):
+        relay(0, i)
+    chain_end(1)
+    attention(1)
+    out_load.wait()
+    for i in range(blocks):
+        settle(0, i)
+    for i in range(blocks):
+        relay(1, i)
+    for i in range(blocks):
+        settle(1, i)
+
+    for h in range(HALVES):
+
+        @pl.when(b == 0)
+        def _():
+            pair_state(h).wait_send()
+
+        @pl.when((b == 1) & has_up)
+        def _():
+            line_state(h).wait_send()
+
+        @pl.when((b == 1) & has_down)
+        def _():
+            back_state(h).wait_send()
+
+        for i in range(blocks):
+            for k in range(tp - 1):
+                normed_copy(h, i, col, k, pair_col).wait_send()
 
     for pieces in phases:
         for piece in pieces:
@@ -232,110 +453,72 @@
                         copy(piece, source, send_peer.at[piece, source], peer).wait_send()
 
 
-def project(seq, tokens, query_weight, key_weight, value_weight, gate_weight):
+def on_device(
+    seq,
+    tp,
+    tokens,
+    query_weight,
+    key_weight,
+    value_weight,
+    gate_weight,
+    decay_rate,
+    norm_gain,
+    out_weight,
+):
     count = tokens.shape[0]
     rows, width = query_weight.shape
     heads = gate_weight.shape[1]
+    half = width // HALVES
+    head_size = width // heads
     wide = rows % 128 == 0
     tok = tokens if wide else tokens.reshape(count, seq, rows).transpose(1, 0, 2)
     gate_t = jnp.pad(gate_weight.T, ((0, 16 - heads), (0, 0)))
+    rate = jnp.pad(decay_rate, (0, 8 - heads))[:, None]
     vmem = pl.BlockSpec(memory_space=pltpu.VMEM)
     hbm = pl.BlockSpec(memory_space=pl.ANY)
     pieces = 3 * HALVES + 1
-    wide_out = jax.ShapeDtypeStruct((count, width), jnp.bfloat16)
+    blocks = count // 256 if count % 256 == 0 else 1
     dma = pltpu.SemaphoreType.DMA
+    deep = head_size * heads // HALVES
+    out_width = out_weight.shape[1]
     return pl.pallas_call(
-        functools.partial(project_kernel, seq, wide),
-        out_shape=(jax.ShapeDtypeStruct((count, 16), jnp.float32), wide_out, wide_out, wide_out),
-        in_specs=[vmem, hbm, hbm, hbm, hbm],
-        out_specs=(vmem, vmem, vmem, vmem),
+        functools.partial(layer_kernel, seq, tp, heads, wide),
+        out_shape=jax.ShapeDtypeStruct((count, out_width), jnp.bfloat16),
+        in_specs=[vmem, vmem, vmem, hbm, hbm, hbm, hbm, hbm],
+        out_specs=vmem,
         scratch_shapes=[
             pltpu.VMEM((seq, 16, rows), jnp.bfloat16),
-            pltpu.VMEM((3 * HALVES, seq, rows, width // HALVES), jnp.bfloat16),
+            pltpu.VMEM((3 * HALVES, seq, rows, half), jnp.bfloat16),
             pltpu.VMEM((count, 16), jnp.float32),
-            pltpu.VMEM((3 * HALVES, count, width // HALVES), jnp.float32),
-            dma((pieces,)),
+            pltpu.VMEM((3 * HALVES, count, half), jnp.float32),
+            pltpu.VMEM(out_weight.shape, jnp.bfloat16),
+            pltpu.VMEM((count, out_width), jnp.float32),
+            pltpu.VMEM((count, 128), jnp.float32),
+            pltpu.VMEM((8, count), jnp.float32),
+            pltpu.VMEM((HALVES, deep + 8, head_size), jnp.float32),
+            pltpu.VMEM((HALVES, deep + 8, head_size), jnp.float32),
+            pltpu.VMEM((HALVES, deep, head_size), jnp.float32),
+            pltpu.VMEM((HALVES, deep, head_size), jnp.float32),
+            pltpu.VMEM((HALVES, tp, count, half), jnp.bfloat16),
+            dma((pieces + 1,)),
             dma((pieces, 3)),
             dma((pieces, seq)),
             dma((pieces, seq)),
             dma((pieces, seq)),
+            dma((3, HALVES)),
+            dma((2, HALVES)),
+            dma((HALVES, blocks, tp - 1)),
+            dma((HALVES, blocks, tp)),
         ],
         compiler_params=pltpu.CompilerParams(
-            collective_id=0, has_side_effects=True, vmem_limit_bytes=60 * 1024 * 1024
+            collective_id=0, has_side_effects=True, vmem_limit_bytes=62 * 1024 * 1024
         ),
-    )(tok, gate_t, key_weight, value_weight, query_weight)
-
-
-def on_device(
-    seq, tokens, query_weight, key_weight, value_weight, gate_weight, decay_rate, norm_gain, out_weight
-):
-    tok_rows = tokens.shape[0]
-    head_count = decay_rate.shape[0]
-    proj_width = query_weight.shape[1]
-    head_size = proj_width // head_count
-    gate_wide, key_proj, value_proj, query_proj = project(
-        seq, tokens, query_weight, key_weight, value_weight, gate_weight
-    )
-    gate_logit = gate_wide[:, :head_count]
-    query_heads = query_proj.reshape(tok_rows, head_count, head_size)
-    key_heads = key_proj.reshape(tok_rows, head_count, head_size)
-    value_per_head = value_proj.reshape(tok_rows, head_count, head_size)
-    log_decay = -decay_rate[None, :] * jax.nn.softplus(gate_logit)
-    within = jnp.cumsum(log_decay, axis=0)
-    block_total = within[-1]
-    key_scaled = (jnp.exp(block_total[None, :] - within)[:, :, None] * key_heads).astype(
-        jnp.bfloat16
-    )
-    shard_local_state = jnp.einsum(
-        "gfw,gfz->fwz", key_scaled, value_per_head, preferred_element_type=jnp.float32
-    )
-    all_totals = lax.all_gather(block_total[None, :], "seq", axis=0, tiled=True)
-    running_sum = jnp.cumsum(all_totals, axis=0)
-    seq_rank = lax.axis_index("seq")
-    before = lax.dynamic_index_in_dim(running_sum, jnp.maximum(seq_rank - 1, 0), 0, keepdims=False)
-    piece = lax.all_gather(shard_local_state[None], "seq", axis=0, tiled=True)
-    piece_rows = piece.shape[0]
-    positions = jnp.arange(piece_rows, dtype=jnp.int32)
-    earlier_ok = (positions < seq_rank)[:, None]
-    factor = jnp.where(
-        earlier_ok, jnp.exp(jnp.where(earlier_ok, before[None, :] - running_sum, 0.0)), 0.0
-    )
-    prefix_state = jnp.sum(factor[:, :, None, None] * piece, axis=0)
-    query_scaled = (jnp.exp(within)[:, :, None] * query_heads).astype(jnp.bfloat16)
-    carried_state = jnp.einsum(
-        "fys,ysu->fyu",
-        query_scaled,
-        prefix_state.astype(jnp.bfloat16),
-        preferred_element_type=jnp.float32,
-    )
-    scores = jnp.einsum("thk,shk->hts", query_heads, key_heads, preferred_element_type=jnp.float32)
-    row_index = lax.broadcasted_iota(jnp.int32, (tok_rows, tok_rows), 0)
-    col_index = lax.broadcasted_iota(jnp.int32, (tok_rows, tok_rows), 1)
-    causal = (col_index <= row_index)[None, :, :]
-    decay_gap = within.T[:, :, None] - within.T[:, None, :]
-    attn = jnp.where(causal, scores * jnp.exp(jnp.where(causal, decay_gap, 0.0)), 0.0).astype(
-        jnp.bfloat16
-    )
-    local_part = jnp.einsum(
-        "hts,shv->thv", attn, value_per_head, preferred_element_type=jnp.float32
-    )
-    head_out = carried_state + local_part
-    mean_square = jnp.mean(head_out * head_out, axis=-1, keepdims=True)
-    normed = (head_out * lax.rsqrt(mean_square + 1e-05)).reshape(tok_rows, proj_width) * norm_gain[
-        None, :
-    ]
-    normed = normed.astype(jnp.bfloat16)
-    mixed = jnp.dot(
-        lax.all_gather(normed, "tp", axis=1, tiled=True),
-        out_weight,
-        preferred_element_type=jnp.float32,
-    )
-    return mixed.astype(jnp.bfloat16)
+    )(tok, rate, norm_gain[None, :], gate_t, key_weight, value_weight, query_weight, out_weight)
 
 
 def solution(mesh):
     return jax.shard_map(
-        functools.partial(on_device, mesh.shape["seq"]),
+        functools.partial(on_device, mesh.shape["seq"], mesh.shape["tp"]),
         mesh=mesh,
         in_specs=(
             P("seq", None),

time: 265 us -> 182 us (0.69)
  waiting for transfers between devices: 50 us -> 0 us
  Pallas kernels: 157 us -> 176 us
  blocking collectives: 17 us -> 0 us
  matrix products: 15.2 us -> 0 us
  between operations: 13.5 us -> 0.01 us
  other arithmetic: 6.93 us -> 0 us
    all_gather x2 -> x0, waiting for transfers between devices: 50 us -> none  [the longest x1 27.2 us: on_device(): lax.all_gather(normed, 'tp', axis=1, tiled=True)]
    pallas_call x1, Pallas kernels: 157 us -> 176 us  [on_device(): pl.pallas_call(functools.partial(layer_kernel, seq, tp, heads, wide), out...]
    all_gather x1 -> x0, blocking collectives: 17 us -> none  [on_device(): all_totals = lax.all_gather(block_total[None, :], 'seq', axis=0, tiled=True)]
    dot_general x4 -> x0, matrix products: 15.2 us -> none  [the longest x1 7.75 us: on_device(): jnp.dot(lax.all_gather(normed, 'tp', axis=1, tiled=True), out_weight, pre...]
  transfers between devices with their start and end apart: 2 -> 0, of which waited for: 2 -> 0; matrix products, arithmetic and copies ran while one was open for 3% -> 0% of each run, Pallas kernels for 0% -> 0%
where the time goes in v2:
time: 182 us
  Pallas kernels  176 us (97%)
  local copies, waits for them, and re-layouts  5.3 us (3%)
    pallas_call x1, Pallas kernels, on_device(): pl.pallas_call(functools.partial(layer_kernel, seq, tp, heads, wide), out...  176 us

profile of v2, /device:TPU:0, one launch (start us, length us, event | category | flops | bytes accessed | tf_op | source)
XLA Modules:
  0.0 181.5 jit_solution(15553653514188273005)
XLA Ops:
  0.0 0.7 pad_bitcast_fusion
  0.7 0.7 copy.9.refs_1_
  1.3 1.3 pad.9.refs_3_
  2.6 176.2 %shard_map.82 = bf16[768,1024]{1,0:T(8,128)(2,1)} custom-call(bf16[768,4096]{1,0:T(8,128)(2,1)} %refs_0_.1, f32[8,1]{1,0:T(8,128)} %copy.9.refs_1_, f32[1,512]{1,0:T(1,128)} %bitcast.5, bf16[16,512]{1,0:T(8,128)(2,1)} %pad.9.refs_3_, bf16[512,512]{1,0:T(8,128)(2,1)} %refs_4_.1, bf16[512,512]{1,0:T(8,128)(2,1)} %refs_5_.1, bf16[512,512]{1,0:T(8,128)(2,1)} %refs_6_.1, ...), custom_call_target="tpu_custom_call" | custom-call | tf_op jit(solution)/shard_map/pallas_call | solution.py:484
  178.8 2.7 %copy.11 = bf16[768,1024]{1,0:T(8,128)(2,1)} copy(bf16[768,1024]{1,0:T(8,128)(2,1)} %shard_map.82) | data formatting | bytes 3145728

commit v3 on v2

--- a/solution.py
+++ b/solution.py
@@ -12,12 +12,12 @@
 
 
 def layer_kernel(seq, tp, heads, wide, *refs):
-    tok_ref, rate_ref, gain_ref, gate_in, key_in, value_in, query_in, out_in = refs[:8]
+    tok_in, rate_ref, gain_ref, gate_in, key_in, value_in, query_in, out_in = refs[:8]
     mixed_ref = refs[8]
     gate_buf, kvq_buf, gate_acc, acc, out_buf, out_acc, wcol, wrow = refs[9:17]
     state_mine, state_peer, state_in, state_next, normed_buf = refs[17:22]
     own_sem, send_own, send_line, send_peer, recv_sem = refs[22:27]
-    state_send, state_recv, normed_send, normed_recv = refs[27:31]
+    state_send, state_recv, normed_send, normed_recv, tok_ref = refs[27:32]
     rows = key_in.shape[0]
     half = key_in.shape[1] // HALVES
     cross = 2
@@ -71,6 +71,8 @@
         )
     for load in loads:
         load.start()
+    tok_load = pltpu.make_async_copy(tok_in, tok_ref, own_sem.at[3 * HALVES + 2])
+    tok_load.start()
     out_load = pltpu.make_async_copy(out_in, out_buf, own_sem.at[3 * HALVES + 1])
     out_load.start()
 
@@ -93,10 +95,13 @@
         )
     pl.semaphore_wait(barrier, 1 + groups + has_up.astype(jnp.int32) + has_down.astype(jnp.int32))
 
-    def send_mine(pieces):
+    def send_across(pieces):
         for piece in pieces:
             loads[piece].wait()
             copy(piece, me, send_own.at[piece, 0], peer).start()
+
+    def send_mine(pieces):
+        for piece in pieces:
 
             @pl.when(has_up)
             def _():
@@ -243,8 +248,8 @@
     def far_pair(g):
         return lax.rem(pair_col + 2 * g, tp)
 
-    def attention(h):
-        for i in range(blocks):
+    def attention(h, which):
+        for i in which:
             t_at = slice(i * block, (i + 1) * block)
             upto = (i + 1) * block
             row = i * block + lax.broadcasted_iota(jnp.int32, (block, upto), 0)
@@ -307,7 +312,12 @@
     steps = 2 * (line - 1)
     for number, pieces in enumerate(phases):
         if number == 0:
-            send_mine(pieces)
+            for piece in pieces:
+                send_across([piece])
+                send_mine([piece])
+            for later in phases[1:]:
+                send_across(later)
+            tok_load.wait()
         for piece in pieces:
             if piece in peer_first:
                 arrive(piece, peer)
@@ -338,14 +348,15 @@
                     def _():
                         copy(piece, source, send_line.at[piece, source], target).start()
 
+                    if piece not in peer_first:
+                        copy(piece, source, send_peer.at[piece, source], peer).start()
+                for piece in pieces:
                     if piece in peer_first:
                         arrive(piece, other)
 
                         @pl.when(onward)
                         def _():
                             copy(piece, other, send_line.at[piece, other], target).start()
-                    else:
-                        copy(piece, source, send_peer.at[piece, source], peer).start()
                 for piece in pieces:
                     multiply(piece, source)
 
@@ -354,6 +365,13 @@
                 @pl.when(t == 2 * (jnp.maximum(a, 1) - 1))
                 def _():
                     chain(number - 1)
+
+            if number == 2:
+                for i in range(blocks):
+
+                    @pl.when(t == 2 * i + 1)
+                    def _():
+                        attention(0, [i])
 
             @pl.when(t == 1)
             def _():
@@ -368,6 +386,9 @@
 
         if number + 1 < len(phases):
             send_mine(phases[number + 1])
+
+        if number == 2:
+            attention(0, [i for i in range(blocks) if 2 * i + 1 >= steps])
 
         @pl.loop(steps - 2, steps)
         def _(t):
@@ -379,12 +400,11 @@
         elif number == 1:
             local_state(1)
             chain_end(0)
-            attention(0)
 
     for i in range(blocks):
         relay(0, i)
     chain_end(1)
-    attention(1)
+    attention(1, range(blocks))
     out_load.wait()
     for i in range(blocks):
         settle(0, i)
@@ -484,7 +504,7 @@
     return pl.pallas_call(
         functools.partial(layer_kernel, seq, tp, heads, wide),
         out_shape=jax.ShapeDtypeStruct((count, out_width), jnp.bfloat16),
-        in_specs=[vmem, vmem, vmem, hbm, hbm, hbm, hbm, hbm],
+        in_specs=[hbm, vmem, vmem, hbm, hbm, hbm, hbm, hbm],
         out_specs=vmem,
         scratch_shapes=[
             pltpu.VMEM((seq, 16, rows), jnp.bfloat16),
@@ -500,7 +520,7 @@
             pltpu.VMEM((HALVES, deep, head_size), jnp.float32),
             pltpu.VMEM((HALVES, deep, head_size), jnp.float32),
             pltpu.VMEM((HALVES, tp, count, half), jnp.bfloat16),
-            dma((pieces + 1,)),
+            dma((pieces + 2,)),
             dma((pieces, 3)),
             dma((pieces, seq)),
             dma((pieces, seq)),
@@ -509,6 +529,7 @@
             dma((2, HALVES)),
             dma((HALVES, blocks, tp - 1)),
             dma((HALVES, blocks, tp)),
+            pltpu.VMEM(tok.shape, jnp.bfloat16),
         ],
         compiler_params=pltpu.CompilerParams(
             collective_id=0, has_side_effects=True, vmem_limit_bytes=62 * 1024 * 1024

time: 182 us -> 168 us (0.923)
  Pallas kernels: 176 us -> 163 us
    pallas_call x1, Pallas kernels: 176 us -> 163 us  [on_device(): pl.pallas_call(functools.partial(layer_kernel, seq, tp, heads, wide), out...]
where the time goes in v3:
time: 168 us
  Pallas kernels  163 us (97%)
  local copies, waits for them, and re-layouts  5.3 us (3%)
    pallas_call x1, Pallas kernels, on_device(): pl.pallas_call(functools.partial(layer_kernel, seq, tp, heads, wide), out...  163 us

profile of v3, /device:TPU:0, one launch (start us, length us, event | category | flops | bytes accessed | tf_op | source)
XLA Modules:
  0.0 168.1 jit_solution(271857598648256661)
XLA Ops:
  0.0 0.7 pad_bitcast_fusion
  0.7 0.7 copy.9.refs_1_
  1.3 1.3 pad.9.refs_3_
  2.6 162.8 %shard_map.82 = bf16[768,1024]{1,0:T(8,128)(2,1)} custom-call(bf16[768,4096]{1,0:T(8,128)(2,1)} %refs_0_.1, f32[8,1]{1,0:T(8,128)} %copy.9.refs_1_, f32[1,512]{1,0:T(1,128)} %bitcast.5, bf16[16,512]{1,0:T(8,128)(2,1)} %pad.9.refs_3_, bf16[512,512]{1,0:T(8,128)(2,1)} %refs_4_.1, bf16[512,512]{1,0:T(8,128)(2,1)} %refs_5_.1, bf16[512,512]{1,0:T(8,128)(2,1)} %refs_6_.1, ...), custom_call_target="tpu_custom_call" | custom-call | tf_op jit(solution)/shard_map/pallas_call | solution.py:504
  165.5 2.7 %copy.11 = bf16[768,1024]{1,0:T(8,128)(2,1)} copy(bf16[768,1024]{1,0:T(8,128)(2,1)} %shard_map.82) | data formatting | bytes 3145728

commit v4 on v3

--- a/solution.py
+++ b/solution.py
@@ -37,6 +37,9 @@
     def buffer(piece, source):
         if piece == 0:
             return gate_buf.at[source]
+        if piece >= 3 * HALVES:
+            at = pl.ds((piece - 3 * HALVES) * (half // 2), half // 2)
+            return kvq_buf.at[3 * HALVES - 1, source, :, at]
         return kvq_buf.at[piece - 1, source]
 
     def tok(source):
@@ -57,7 +60,7 @@
     def arrive(piece, source):
         copy(piece, source, send_own.at[piece, 0], peer).wait_recv()
 
-    phases = [[1, 0, 2, 3], [4, 5], [6]]
+    phases = [[1, 0, 2, 3], [4, 5], [6, 7]]
     peer_first = (1,)
 
     loads = [pltpu.make_async_copy(gate_in, gate_buf.at[me], own_sem.at[0])]
@@ -97,7 +100,8 @@
 
     def send_across(pieces):
         for piece in pieces:
-            loads[piece].wait()
+            if piece <= 3 * HALVES:
+                loads[piece].wait()
             copy(piece, me, send_own.at[piece, 0], peer).start()
 
     def send_mine(pieces):
@@ -117,9 +121,10 @@
             gate_acc[...] += lax.dot_general(
                 x, gate_buf[source], (((1,), (1,)), ((), ())), preferred_element_type=jnp.float32
             )
-        else:
-            acc[piece - 1] += jnp.dot(
-                x, kvq_buf[piece - 1, source], preferred_element_type=jnp.float32
+        elif piece != 3 * HALVES:
+            index = min(piece, 3 * HALVES) - 1
+            acc[index] += jnp.dot(
+                x, kvq_buf[index, source], preferred_element_type=jnp.float32
             )
 
     def step_of(t):
@@ -333,62 +338,81 @@
         for piece in pieces:
             multiply(piece, me)
 
-        @pl.loop(0, steps)
-        def _(t):
-            origin, valid, onward, target = step_of(t)
-            source = origin * cross + b
-            other = origin * cross + (1 - b)
-
-            @pl.when(valid)
-            def _():
-                for piece in pieces:
-                    arrive(piece, source)
-
-                    @pl.when(onward)
+        @pl.loop(1, line)
+        def _(d):
+            sides = [step_of(2 * (d - 1) + way) for way in (0, 1)]
+
+            for piece in pieces:
+                for origin, valid, onward, target in sides:
+
+                    @pl.when(valid)
                     def _():
-                        copy(piece, source, send_line.at[piece, source], target).start()
-
-                    if piece not in peer_first:
-                        copy(piece, source, send_peer.at[piece, source], peer).start()
-                for piece in pieces:
-                    if piece in peer_first:
-                        arrive(piece, other)
+                        source = origin * cross + b
+                        arrive(piece, source)
 
                         @pl.when(onward)
                         def _():
-                            copy(piece, other, send_line.at[piece, other], target).start()
-                for piece in pieces:
-                    multiply(piece, source)
+                            copy(piece, source, send_line.at[piece, source], target).start()
+
+                        if piece not in peer_first:
+                            copy(piece, source, send_peer.at[piece, source], peer).start()
+
+            for piece in pieces:
+                if piece in peer_first:
+                    for origin, valid, onward, target in sides:
+
+                        @pl.when(valid)
+                        def _():
+                            other = origin * cross + (1 - b)
+                            arrive(piece, other)
+
+                            @pl.when(onward)
+                            def _():
+                                copy(piece, other, send_line.at[piece, other], target).start()
+
+            for way in (0, 1):
+                origin, valid, _, _ = sides[way]
+
+                @pl.when(valid)
+                def _():
+                    for piece in pieces:
+                        multiply(piece, origin * cross + b)
 
             if number >= 1:
 
-                @pl.when(t == 2 * (jnp.maximum(a, 1) - 1))
+                @pl.when(d == jnp.maximum(a, 1))
                 def _():
                     chain(number - 1)
 
             if number == 2:
+
+                @pl.when(d == 1)
+                def _():
+                    chain_end(0)
+
                 for i in range(blocks):
 
-                    @pl.when(t == 2 * i + 1)
+                    @pl.when(d == i + 1)
                     def _():
                         attention(0, [i])
 
-            @pl.when(t == 1)
+            @pl.when(d == 1)
             def _():
                 for piece in pieces:
                     if piece not in peer_first:
                         arrive(piece, peer)
                     multiply(piece, peer)
 
-            @pl.when(t >= 2)
-            def _():
-                from_peer(pieces, t - 2)
+            @pl.when(d >= 2)
+            def _():
+                from_peer(pieces, 2 * (d - 2))
+                from_peer(pieces, 2 * (d - 2) + 1)
 
         if number + 1 < len(phases):
             send_mine(phases[number + 1])
 
         if number == 2:
-            attention(0, [i for i in range(blocks) if 2 * i + 1 >= steps])
+            attention(0, range(line - 1, blocks))
 
         @pl.loop(steps - 2, steps)
         def _(t):
@@ -399,7 +423,6 @@
             local_state(0)
         elif number == 1:
             local_state(1)
-            chain_end(0)
 
     for i in range(blocks):
         relay(0, i)
@@ -496,7 +519,7 @@
     rate = jnp.pad(decay_rate, (0, 8 - heads))[:, None]
     vmem = pl.BlockSpec(memory_space=pltpu.VMEM)
     hbm = pl.BlockSpec(memory_space=pl.ANY)
-    pieces = 3 * HALVES + 1
+    pieces = 3 * HALVES + 2
     blocks = count // 256 if count % 256 == 0 else 1
     dma = pltpu.SemaphoreType.DMA
     deep = head_size * heads // HALVES

time: 168 us -> 165 us (0.982)
  Pallas kernels: 163 us -> 160 us
    pallas_call x1, Pallas kernels: 163 us -> 160 us  [on_device(): pl.pallas_call(functools.partial(layer_kernel, seq, tp, heads, wide), out...]
where the time goes in v4:
time: 165 us
  Pallas kernels  160 us (97%)
  local copies, waits for them, and re-layouts  5.3 us (3%)
    pallas_call x1, Pallas kernels, on_device(): pl.pallas_call(functools.partial(layer_kernel, seq, tp, heads, wide), out...  160 us

profile of v4, /device:TPU:0, one launch (start us, length us, event | category | flops | bytes accessed | tf_op | source)
XLA Modules:
  0.0 165.0 jit_solution(12790217770542826248)
XLA Ops:
  0.0 0.7 pad_bitcast_fusion
  0.7 0.7 copy.9.refs_1_
  1.3 1.3 pad.9.refs_3_
  2.6 159.7 %shard_map.82 = bf16[768,1024]{1,0:T(8,128)(2,1)} custom-call(bf16[768,4096]{1,0:T(8,128)(2,1)} %refs_0_.1, f32[8,1]{1,0:T(8,128)} %copy.9.refs_1_, f32[1,512]{1,0:T(1,128)} %bitcast.5, bf16[16,512]{1,0:T(8,128)(2,1)} %pad.9.refs_3_, bf16[512,512]{1,0:T(8,128)(2,1)} %refs_4_.1, bf16[512,512]{1,0:T(8,128)(2,1)} %refs_5_.1, bf16[512,512]{1,0:T(8,128)(2,1)} %refs_6_.1, ...), custom_call_target="tpu_custom_call" | custom-call | tf_op jit(solution)/shard_map/pallas_call | solution.py:527
  162.3 2.7 %copy.11 = bf16[768,1024]{1,0:T(8,128)(2,1)} copy(bf16[768,1024]{1,0:T(8,128)(2,1)} %shard_map.82) | data formatting | bytes 3145728
